TPU v7x, 64 devices: a 2x2x8 block of a 4x4x8 slice. The times are simulated.
64 devices in a mesh: graph: 4 (over x, y), nodes: 16 (over z, core).
Axes of the slice: x: 2, y: 2, z: 8, core: 2. Of those that a mesh axis runs over, the one named last changes fastest.
The devices are a block of a 4x4x8 slice.
Arguments:
- node_feats: bfloat16 [98304, 1433], P(('graph', 'nodes')), parts along dimension 0
- a_int: bfloat16 [98304, 1536], P(('graph', 'nodes')), parts along dimension 0
- a_halo: bfloat16 [98304, 512], P(('graph', 'nodes')), parts along dimension 0
- send_idx: int32 [256, 128], P(('graph', 'nodes')), parts along dimension 0
- w_first: bfloat16 [1433, 16], replicated
- w_second: bfloat16 [16, 7], replicated
- grad_out: bfloat16 [98304, 7], P(('graph', 'nodes')), parts along dimension 0
Outputs:
- output 1: float32 [5732, 16], P('graph'), parts along dimension 0
- output 2: float32 [64, 7], P('graph'), parts along dimension 0
- output 3: float32 [98304, 1433], P(('graph', 'nodes')), parts along dimension 0
There are 4 independent parts. A program takes and returns all parts, laid end to end along the dimension named above; an argument that names none is the same for every part.
All inputs are finite; a program needn't handle non-finite values.
Results may differ from a plain program's by a relative error of at most 0.00548394.
Values are sent between devices in bfloat16 or wider.
A program may use at most 768 MiB of HBM per device.

v0:
```python
import jax
import jax.numpy as jnp
from jax import lax
from jax.sharding import PartitionSpec as P


def link_offsets(num_links):
    return [(link // 2 + 1) * (1 - 2 * (link % 2)) for link in range(num_links)]


def shift_pairs(axis_size, offset):
    return [(source, (source + offset) % axis_size) for source in range(axis_size)]


def contract_rows(left_rows, right_rows):
    return lax.dot_general(left_rows, right_rows, (((0,), (0,)), ((), ())), preferred_element_type=jnp.float32)


def halo_rows(features, send_idx, axis_size):
    sent_rows = jnp.take(features, send_idx, axis=0)
    received = [lax.ppermute(sent_rows[link], "nodes", shift_pairs(axis_size, offset)) for link, offset in enumerate(link_offsets(send_idx.shape[0]))]
    return jnp.concatenate(received, axis=0)


def aggregate(a_int, a_halo, features, send_idx, axis_size):
    remote = halo_rows(features, send_idx, axis_size)
    return jnp.dot(a_int, features, preferred_element_type=jnp.float32) + jnp.dot(a_halo, remote, preferred_element_type=jnp.float32)


def aggregate_back(a_int, a_halo, grad_rows, send_idx, axis_size):
    num_slots = send_idx.shape[1]
    inner_sum = contract_rows(a_int, grad_rows)
    outward = contract_rows(a_halo, grad_rows).astype(jnp.bfloat16)
    received = [lax.ppermute(outward[link * num_slots:(link + 1) * num_slots], "nodes", shift_pairs(axis_size, -offset)) for link, offset in enumerate(link_offsets(send_idx.shape[0]))]
    returned = jnp.concatenate(received, axis=0).astype(jnp.float32)
    return inner_sum.at[send_idx.reshape(-1)].add(returned)


def solution(mesh):
    axis_size = mesh.shape["nodes"]
    row_spec = P(("graph", "nodes"), None)
    replicated = P(None, None)
    part_spec = P("graph", None)

    def device_step(node_feats, a_int, a_halo, send_idx, w_first, w_second, grad_out):
        z_first = aggregate(a_int, a_halo, node_feats, send_idx, axis_size).astype(jnp.bfloat16)
        hidden = jnp.maximum(jnp.dot(z_first, w_first, preferred_element_type=jnp.float32), 0.0).astype(jnp.bfloat16)
        z_second = aggregate(a_int, a_halo, hidden, send_idx, axis_size).astype(jnp.bfloat16)
        dw_second = lax.psum(contract_rows(z_second, grad_out), "nodes")
        dz_second = lax.dot_general(grad_out, w_second, (((1,), (1,)), ((), ())), preferred_element_type=jnp.float32).astype(jnp.bfloat16)
        d_hidden = aggregate_back(a_int, a_halo, dz_second, send_idx, axis_size)
        grad_pre = jnp.where(hidden > 0, d_hidden, 0.0).astype(jnp.bfloat16)
        dw_first = lax.psum(contract_rows(z_first, grad_pre), "nodes")
        dz_first = lax.dot_general(grad_pre, w_first, (((1,), (1,)), ((), ())), preferred_element_type=jnp.float32).astype(jnp.bfloat16)
        grad_feats = aggregate_back(a_int, a_halo, dz_first, send_idx, axis_size)
        return dw_first, dw_second, grad_feats

    return jax.shard_map(device_step, mesh=mesh, in_specs=(row_spec, row_spec, row_spec, row_spec, replicated, replicated, row_spec), out_specs=(part_spec, part_spec, row_spec), check_vma=False)
```

profile of v0, /device:TPU:21, one launch (start us, length us, event | category | flops | bytes accessed | tf_op | source)
XLA Modules:
  0.0 217.9 jit_solution(16928921179518465323)
XLA Ops:
  7.2 0.0 copy-start
  7.2 0.1 all-reduce.2.cloned.1.call-start
  7.3 1.0 convolution_convert_fusion.2
  8.3 0.3 copy-done
  8.6 0.3 fusion.12
  8.9 4.7 %collective-permute-start.4 = (bf16[128,16]{0,1:T(8,128)(2,1)S(1)}, bf16[128,16]{0,1:T(8,128)(2,1)S(1)}, u32[]{:S(2)}, u32[]{:S(2)}) collective-permute-start(bf16[128,16]{0,1:T(8,128)(2,1)S(1)} %get-tuple-element.21), channel_id=1, source_target_pairs={{0,15},{1,0},{2,1},{3,2},{4,3},{5,4},{6,5},{7,6},{8,7},{9,8},{10,9... | collective-permute-start | bytes 12296 | tf_op jit(solution)/shard_map/ppermute | solution.py:34
  13.6 0.0 collective-permute-start.7
  13.6 3.8 %collective-permute-start.6 = (bf16[128,16]{0,1:T(8,128)(2,1)S(1)}, bf16[128,16]{0,1:T(8,128)(2,1)S(1)}, u32[]{:S(2)}, u32[]{:S(2)}) collective-permute-start(bf16[128,16]{0,1:T(8,128)(2,1)S(1)} %get-tuple-element.23), channel_id=1, source_target_pairs={{0,14},{1,15},{2,0},{3,1},{4,2},{5,3},{6,4},{7,5},{8,6},{9,7},{10,... | collective-permute-start | bytes 12296 | tf_op jit(solution)/shard_map/ppermute | solution.py:34
  17.4 0.7 compare_and_fusion
  18.1 0.7 fusion.27
  18.7 6.6 %copy.18 = bf16[1536,1433]{1,0:T(8,128)(2,1)} copy(bf16[1536,1433]{0,1:T(8,128)(2,1)} %param.7) | data formatting | bytes 8804352 | tf_op args[0]
  25.3 6.5 %gather_fusion = bf16[512,1433]{1,0:T(8,128)(2,1)S(1)} fusion(bf16[1536,1433]{1,0:T(8,128)(2,1)} %copy.18, s32[1024]{0:T(1024)S(1)} %pad_clamp_fusion), kind=kCustom, calls=%fused_computation | custom fusion | bytes 2936832 | tf_op jit(solution)/shard_map/jit(_take)/gather | solution.py:20
  31.8 0.2 broadcast_select_fusion
  32.1 1.2 slice_bitcast_fusion.3
  33.3 1.4 collective-permute-start
  34.7 4.2 %collective-permute-start.3 = (bf16[128,1433]{1,0:T(8,128)(2,1)}, bf16[128,1433]{1,0:T(8,128)(2,1)}, u32[]{:S(2)}, u32[]{:S(2)}) collective-permute-start(bf16[128,1433]{1,0:T(8,128)(2,1)} %get-tuple-element.10), channel_id=1, source_target_pairs={{0,14},{1,15},{2,0},{3,1},{4,2},{5,3},{6,4},{7,5},{8,6},{9,7},{10,... | collective-permute-start | bytes 1100552 | tf_op jit(solution)/shard_map/ppermute | solution.py:21
  38.9 12.4 %fusion.34 = f32[1536,1433]{0,1:T(8,128)} fusion(bf16[1536,1536]{1,0:T(8,128)(2,1)} %param.8, bf16[1536,1433]{0,1:T(8,128)(2,1)} %param.7), kind=kOutput, calls=%fused_computation.56 | convolution fusion | flops 6761742336 | bytes 17925120 | tf_op jit(solution)/shard_map/dot_general | solution.py:27
  51.2 0.0 collective-permute-start.2
  51.2 0.0 collective-permute-done.7
  51.3 0.1 collective-permute-start.1
  51.4 0.7 convolution_bitcast_fusion.1
  52.1 0.0 collective-permute-done.6
  52.1 1.7 collective-permute-start.5
  53.8 0.3 copy.19
  54.1 5.9 %collective-permute-done.5 = bf16[128,16]{0,1:T(8,128)(2,1)S(1)} collective-permute-done((bf16[128,16]{0,1:T(8,128)(2,1)S(1)}, bf16[128,16]{0,1:T(8,128)(2,1)S(1)}, u32[]{:S(2)}, u32[]{:S(2)}) %collective-permute-start.5) | collective-permute-done | bytes 4128 | tf_op jit(solution)/shard_map/ppermute | solution.py:34
  59.9 0.1 copy.20
  60.1 0.0 slice-start.2
  60.1 4.3 %scatter_fusion = f32[1536,16]{1,0:T(8,128)S(1)} fusion(f32[1536,16]{1,0:T(8,128)S(1)} %copy.19, s32[512]{0:T(512)S(1)} %bitcast.64, f32[512,16]{1,0:T(8,128)S(1)} %copy.20), kind=kCustom, calls=%fused_computation.2 | custom fusion | flops 8192 | bytes 100352 | tf_op jit(solution)/shard_map/scatter-add | solution.py:36
  64.3 0.1 copy.21
  64.5 0.0 collective-permute-done.3
  64.5 0.0 collective-permute-done.2
  64.5 6.9 %fusion = bf16[1536,1433]{0,1:T(8,128)(2,1)S(1)} fusion(f32[1536,1433]{0,1:T(8,128)} %fusion.34, bf16[1536,512]{1,0:T(8,128)(2,1)S(1)} %copy-done, bf16[128,1433]{1,0:T(8,128)(2,1)} %collective-permute-done.3, bf16[128,1433]{1,0:T(8,128)(2,1)} %collective-permute-done.2, bf16[128,1433]{1,0:T(8,128)(2,1)} %collective-permute-done.1, ...), kind=kOutput, calls=%fused_computation.5 | convolution fusion | flops 2264185856 | bytes 16246784 | tf_op jit(solution)/shard_map/dot_general | solution.py:27
  71.4 2.0 copy-done.1
  73.4 0.7 fusion.2
  74.1 1.3 fusion.35
  75.5 0.2 copy.22
  75.7 0.0 slice-start.4
  75.7 1.4 convolution_convert_fusion
  77.1 0.0 slice-start.5
  77.1 3.7 %fusion.1 = bf16[512,1433]{0,1:T(8,128)(2,1)} fusion(bf16[1536,1433]{0,1:T(8,128)(2,1)S(1)} %convolution_convert_fusion, bf16[1536,512]{1,0:T(8,128)(2,1)S(1)} %copy-done), kind=kOutput, calls=%fused_computation.9 | convolution fusion | flops 2254647808 | bytes 7442432 | tf_op jit(solution)/shard_map/dot_general | solution.py:16
  80.8 9.6 %convolution_bitcast_fusion = f32[1536,1433]{0,1:T(8,128)} fusion(bf16[1536,1433]{0,1:T(8,128)(2,1)S(1)} %convolution_convert_fusion, bf16[1536,1536]{1,0:T(8,128)(2,1)S(1)} %bitcast.60), kind=kOutput, calls=%fused_computation.6 | convolution fusion | flops 6761742336 | bytes 17925120 | tf_op jit(solution)/shard_map/dot_general | solution.py:16
  90.4 1.3 gather_fusion.1
  91.7 0.1 copy.23
  91.8 2.5 %collective-permute-start.8 = (bf16[128,16]{0,1:T(8,128)(2,1)S(1)}, bf16[128,16]{0,1:T(8,128)(2,1)S(1)}, u32[]{:S(2)}, u32[]{:S(2)}) collective-permute-start(bf16[128,16]{0,1:T(8,128)(2,1)S(1)} %get-tuple-element.17), channel_id=1, source_target_pairs={{0,1},{1,2},{2,3},{3,4},{4,5},{5,6},{6,7},{7,8},{8,9},{9,10},{10,1... | collective-permute-start | bytes 12296 | tf_op jit(solution)/shard_map/ppermute | solution.py:21
  94.3 2.2 %collective-permute-start.11 = (bf16[128,16]{0,1:T(8,128)(2,1)S(1)}, bf16[128,16]{0,1:T(8,128)(2,1)S(1)}, u32[]{:S(2)}, u32[]{:S(2)}) collective-permute-start(bf16[128,16]{0,1:T(8,128)(2,1)S(1)} %get-tuple-element.18), channel_id=1, source_target_pairs={{0,14},{1,15},{2,0},{3,1},{4,2},{5,3},{6,4},{7,5},{8,6},{9,7},{10,... | collective-permute-start | bytes 12296 | tf_op jit(solution)/shard_map/ppermute | solution.py:21
  96.5 0.0 collective-permute-start.10
  96.6 0.0 collective-permute-start.9
  96.6 2.3 %fusion.32 = (bf16[128,1433]{0,1:T(8,128)(2,1)}, bf16[128,1433]{0,1:T(8,128)(2,1)}, bf16[128,1433]{0,1:T(8,128)(2,1)S(1)}, bf16[128,1433]{0,1:T(8,128)(2,1)S(1)}) fusion(bf16[512,1433]{0,1:T(8,128)(2,1)} %fusion.1), kind=kLoop, calls=%fused_computation.54 | loop fusion | bytes 2934784 | tf_op jit(solution)/shard_map/slice | solution.py:34
  98.9 3.1 %collective-permute-start.12 = (bf16[128,1433]{0,1:T(8,128)(2,1)}, bf16[128,1433]{0,1:T(8,128)(2,1)S(1)}, u32[]{:S(2)}, u32[]{:S(2)}) collective-permute-start(bf16[128,1433]{0,1:T(8,128)(2,1)} %get-tuple-element.13), channel_id=1, source_target_pairs={{0,15},{1,0},{2,1},{3,2},{4,3},{5,4},{6,5},{7,6},{8,7},{9,8},{10,9... | collective-permute-start | bytes 1100552 | tf_op jit(solution)/shard_map/ppermute | solution.py:34
  101.9 0.0 collective-permute-done.8
  101.9 0.0 collective-permute-start.15
  101.9 2.7 %collective-permute-start.14 = (bf16[128,1433]{0,1:T(8,128)(2,1)S(1)}, bf16[128,1433]{0,1:T(8,128)(2,1)}, u32[]{:S(2)}, u32[]{:S(2)}) collective-permute-start(bf16[128,1433]{0,1:T(8,128)(2,1)S(1)} %get-tuple-element.15), channel_id=1, source_target_pairs={{0,14},{1,15},{2,0},{3,1},{4,2},{5,3},{6,4},{7,5},{8,6},{9,7},{10,... | collective-permute-start | bytes 1100552 | tf_op jit(solution)/shard_map/ppermute | solution.py:34
  104.6 4.2 %fusion.31 = f32[1433,16]{0,1:T(8,128)} fusion(bf16[1536,1433]{0,1:T(8,128)(2,1)} %copy-done.1, bf16[1536,16]{0,1:T(8,128)(2,1)S(1)} %copy.21, bf16[1536,16]{0,1:T(8,128)(2,1)S(1)} %fusion.2), kind=kOutput, calls=%fused_computation.53 | convolution fusion | flops 70533120 | bytes 4592192 | tf_op jit(solution)/shard_map/dot_general | solution.py:16
  108.8 0.1 all-reduce.2.cloned.1.call-update
  108.8 0.0 copy-start.3
  108.9 9.5 %copy.24 = f32[1536,1433]{1,0:T(8,128)} copy(f32[1536,1433]{0,1:T(8,128)} %convolution_bitcast_fusion) | data formatting | bytes 17608704 | tf_op jit(solution)/shard_map/dot_general | solution.py:16
  118.4 0.6 fusion.11
  119.0 24.2 %psum.15 = f32[16,7]{0,1:T(8,128)} all-reduce(f32[16,7]{0,1:T(8,128)S(1)} %fusion.11), channel_id=1, replica_groups=mesh['graph'=4,'nodes'=16] {'nodes'}, use_global_device_ids=true, to_apply=%region_2.3 | all-reduce | flops 112 | bytes 896 | tf_op jit(solution)/shard_map/psum | solution.py:49
  143.2 3.0 %maximum_convert_fusion = f32[512,1433]{0,1:T(8,128)} fusion(bf16[128,1433]{0,1:T(8,128)(2,1)} %collective-permute-done.15, bf16[128,1433]{0,1:T(8,128)(2,1)} %collective-permute-done.14, bf16[128,1433]{0,1:T(8,128)(2,1)} %collective-permute-done.13, bf16[128,1433]{0,1:T(8,128)(2,1)S(1)} %collective-permute-done.12), kind=kLoop, calls=%fused_computation.24 | loop fusion | flops 5869568 | bytes 4402176 | tf_op jit(solution)/shard_map/convert_element_type | solution.py:35
  146.2 3.5 %copy.25 = f32[512,1433]{1,0:T(8,128)} copy(f32[512,1433]{0,1:T(8,128)} %maximum_convert_fusion) | data formatting | bytes 5869568 | tf_op jit(solution)/shard_map/convert_element_type | solution.py:35
  149.7 14.1 %scatter_fusion.1 = f32[1536,1433]{1,0:T(8,128)} fusion(f32[1536,1433]{1,0:T(8,128)} %copy.24, s32[512]{0:T(512)S(1)} %bitcast.65, f32[512,1433]{1,0:T(8,128)} %copy.25), kind=kCustom, calls=%fused_computation.3 | custom fusion | flops 733696 | bytes 8806400 | tf_op jit(solution)/shard_map/scatter-add | solution.py:36
  163.8 9.3 %copy.26 = f32[1536,1433]{0,1:T(8,128)} copy(f32[1536,1433]{1,0:T(8,128)} %scatter_fusion.1) | data formatting | bytes 17608704
  173.1 36.4 %all-reduce.2.cloned.1.call-done = f32[1433,16]{0,1:T(8,128)} async-done(((f32[1433,16]{0,1:T(8,128)}), f32[1433,16]{0,1:T(8,128)}) %all-reduce.2.cloned.1.call-update) | async-done | bytes 91728 | tf_op jit(solution)/shard_map/psum | solution.py:53
  209.5 1.5 copy.30
  (35 shorter events, 0.1 us)
Async XLA Ops:
  7.2 1.4 copy-start
  7.2 202.3 %all-reduce.2.cloned.1.call-start = ((), (), s32[]{:S(2)}) async-start(), calls=%async_computation | async-start | bytes 196608 | tf_op jit(solution)/shard_map/psum | solution.py:53
  8.9 42.3 %collective-permute-start.4 = (bf16[128,16]{0,1:T(8,128)(2,1)S(1)}, bf16[128,16]{0,1:T(8,128)(2,1)S(1)}, u32[]{:S(2)}, u32[]{:S(2)}) collective-permute-start(bf16[128,16]{0,1:T(8,128)(2,1)S(1)} %get-tuple-element.21), channel_id=1, source_target_pairs={{0,15},{1,0},{2,1},{3,2},{4,3},{5,4},{6,5},{7,6},{8,7},{9,8},{10,9... | collective-permute-start | bytes 12296 | tf_op jit(solution)/shard_map/ppermute | solution.py:34
  13.6 37.7 %collective-permute-start.7 = (bf16[128,16]{0,1:T(8,128)(2,1)S(1)}, bf16[128,16]{0,1:T(8,128)(2,1)S(1)}, u32[]{:S(2)}, u32[]{:S(2)}) collective-permute-start(bf16[128,16]{0,1:T(8,128)(2,1)S(1)} %get-tuple-element.22), channel_id=1, source_target_pairs={{0,2},{1,3},{2,4},{3,5},{4,6},{5,7},{6,8},{7,9},{8,10},{9,11},{10,... | collective-permute-start | bytes 12296 | tf_op jit(solution)/shard_map/ppermute | solution.py:34
  13.6 38.5 %collective-permute-start.6 = (bf16[128,16]{0,1:T(8,128)(2,1)S(1)}, bf16[128,16]{0,1:T(8,128)(2,1)S(1)}, u32[]{:S(2)}, u32[]{:S(2)}) collective-permute-start(bf16[128,16]{0,1:T(8,128)(2,1)S(1)} %get-tuple-element.23), channel_id=1, source_target_pairs={{0,14},{1,15},{2,0},{3,1},{4,2},{5,3},{6,4},{7,5},{8,6},{9,7},{10,... | collective-permute-start | bytes 12296 | tf_op jit(solution)/shard_map/ppermute | solution.py:34
  33.3 31.2 %collective-permute-start = (bf16[128,1433]{1,0:T(8,128)(2,1)}, bf16[128,1433]{1,0:T(8,128)(2,1)}, u32[]{:S(2)}, u32[]{:S(2)}) collective-permute-start(bf16[128,1433]{1,0:T(8,128)(2,1)} %get-tuple-element.9), channel_id=1, source_target_pairs={{0,1},{1,2},{2,3},{3,4},{4,5},{5,6},{6,7},{7,8},{8,9},{9,10},{10,1... | collective-permute-start | bytes 1100552 | tf_op jit(solution)/shard_map/ppermute | solution.py:21
  34.7 16.6 %slice-start = ((s8[4718592]{0:T(1024)(128)(4,1)}), s8[4194304]{0:T(1024)(128)(4,1)S(1)}, s32[]{:S(2)}) async-start(s8[4718592]{0:T(1024)(128)(4,1)} %bitcast.55), calls=%async_computation.1 | async-start | bytes 8388608
  34.7 16.6 %slice-start.1 = ((s8[4718592]{0:T(1024)(128)(4,1)}), s8[524288]{0:T(1024)(128)(4,1)S(1)}, s32[]{:S(2)}) async-start(s8[4718592]{0:T(1024)(128)(4,1)} %bitcast.55), calls=%async_computation.2 | async-start | bytes 1048576
  34.7 29.8 %collective-permute-start.3 = (bf16[128,1433]{1,0:T(8,128)(2,1)}, bf16[128,1433]{1,0:T(8,128)(2,1)}, u32[]{:S(2)}, u32[]{:S(2)}) collective-permute-start(bf16[128,1433]{1,0:T(8,128)(2,1)} %get-tuple-element.10), channel_id=1, source_target_pairs={{0,14},{1,15},{2,0},{3,1},{4,2},{5,3},{6,4},{7,5},{8,6},{9,7},{10,... | collective-permute-start | bytes 1100552 | tf_op jit(solution)/shard_map/ppermute | solution.py:21
  51.2 2.6 %copy-start.4 = (s32[4,128]{1,0:T(4,128)S(1)}, s32[4,128]{1,0:T(4,128)}, u32[]{:S(2)}) copy-start(s32[4,128]{1,0:T(4,128)} %param.10) | copy-start | bytes 6148
  51.2 13.3 %collective-permute-start.2 = (bf16[128,1433]{1,0:T(8,128)(2,1)}, bf16[128,1433]{1,0:T(8,128)(2,1)}, u32[]{:S(2)}, u32[]{:S(2)}) collective-permute-start(bf16[128,1433]{1,0:T(8,128)(2,1)} %get-tuple-element.11), channel_id=1, source_target_pairs={{0,2},{1,3},{2,4},{3,5},{4,6},{5,7},{6,8},{7,9},{8,10},{9,11},{10,... | collective-permute-start | bytes 1100552 | tf_op jit(solution)/shard_map/ppermute | solution.py:21
  51.3 13.3 %collective-permute-start.1 = (bf16[128,1433]{1,0:T(8,128)(2,1)}, bf16[128,1433]{1,0:T(8,128)(2,1)}, u32[]{:S(2)}, u32[]{:S(2)}) collective-permute-start(bf16[128,1433]{1,0:T(8,128)(2,1)} %get-tuple-element.12), channel_id=1, source_target_pairs={{0,15},{1,0},{2,1},{3,2},{4,3},{5,4},{6,5},{7,6},{8,7},{9,8},{10,9... | collective-permute-start | bytes 1100552 | tf_op jit(solution)/shard_map/ppermute | solution.py:21
  52.1 7.8 %collective-permute-start.5 = (bf16[128,16]{0,1:T(8,128)(2,1)S(1)}, bf16[128,16]{0,1:T(8,128)(2,1)S(1)}, u32[]{:S(2)}, u32[]{:S(2)}) collective-permute-start(bf16[128,16]{0,1:T(8,128)(2,1)S(1)} %get-tuple-element.24), channel_id=1, source_target_pairs={{0,1},{1,2},{2,3},{3,4},{4,5},{5,6},{6,7},{7,8},{8,9},{9,10},{10,1... | collective-permute-start | bytes 12296 | tf_op jit(solution)/shard_map/ppermute | solution.py:34
  60.1 14.1 %slice-start.2 = ((s8[4718592]{0:T(1024)(128)(4,1)}), s8[524288]{0:T(1024)(128)(4,1)S(1)}, s32[]{:S(2)}) async-start(s8[4718592]{0:T(1024)(128)(4,1)} %bitcast.57), calls=%async_computation.3 | async-start | bytes 1048576
  64.5 9.0 %copy-start.2 = (bf16[1433,16]{0,1:T(8,128)(2,1)S(1)}, bf16[1433,16]{0,1:T(8,128)(2,1)}, u32[]{:S(2)}) copy-start(bf16[1433,16]{0,1:T(8,128)(2,1)} %param.11) | copy-start | bytes 137572
  64.5 9.7 %slice-start.3 = ((s8[4718592]{0:T(1024)(128)(4,1)}), s8[4194304]{0:T(1024)(128)(4,1)S(1)}, s32[]{:S(2)}) async-start(s8[4718592]{0:T(1024)(128)(4,1)} %bitcast.57), calls=%async_computation.4 | async-start | bytes 8388608
  71.4 2.1 copy-start.1
  75.7 5.1 %slice-start.4 = ((s8[4718592]{0:T(1024)(128)(4,1)}), s8[4194304]{0:T(1024)(128)(4,1)S(1)}, s32[]{:S(2)}) async-start(s8[4718592]{0:T(1024)(128)(4,1)} %bitcast.59), calls=%async_computation.5 | async-start | bytes 8388608
  77.1 3.7 %slice-start.5 = ((s8[4718592]{0:T(1024)(128)(4,1)}), s8[524288]{0:T(1024)(128)(4,1)S(1)}, s32[]{:S(2)}) async-start(s8[4718592]{0:T(1024)(128)(4,1)} %bitcast.59), calls=%async_computation.6 | async-start | bytes 1048576
  91.8 10.1 %collective-permute-start.8 = (bf16[128,16]{0,1:T(8,128)(2,1)S(1)}, bf16[128,16]{0,1:T(8,128)(2,1)S(1)}, u32[]{:S(2)}, u32[]{:S(2)}) collective-permute-start(bf16[128,16]{0,1:T(8,128)(2,1)S(1)} %get-tuple-element.17), channel_id=1, source_target_pairs={{0,1},{1,2},{2,3},{3,4},{4,5},{5,6},{6,7},{7,8},{8,9},{9,10},{10,1... | collective-permute-start | bytes 12296 | tf_op jit(solution)/shard_map/ppermute | solution.py:21
  94.3 7.6 %collective-permute-start.11 = (bf16[128,16]{0,1:T(8,128)(2,1)S(1)}, bf16[128,16]{0,1:T(8,128)(2,1)S(1)}, u32[]{:S(2)}, u32[]{:S(2)}) collective-permute-start(bf16[128,16]{0,1:T(8,128)(2,1)S(1)} %get-tuple-element.18), channel_id=1, source_target_pairs={{0,14},{1,15},{2,0},{3,1},{4,2},{5,3},{6,4},{7,5},{8,6},{9,7},{10,... | collective-permute-start | bytes 12296 | tf_op jit(solution)/shard_map/ppermute | solution.py:21
  96.5 8.1 %collective-permute-start.10 = (bf16[128,16]{0,1:T(8,128)(2,1)S(1)}, bf16[128,16]{0,1:T(8,128)(2,1)S(1)}, u32[]{:S(2)}, u32[]{:S(2)}) collective-permute-start(bf16[128,16]{0,1:T(8,128)(2,1)S(1)} %get-tuple-element.19), channel_id=1, source_target_pairs={{0,2},{1,3},{2,4},{3,5},{4,6},{5,7},{6,8},{7,9},{8,10},{9,11},{10,... | collective-permute-start | bytes 12296 | tf_op jit(solution)/shard_map/ppermute | solution.py:21
  96.6 21.8 %collective-permute-start.9 = (bf16[128,16]{0,1:T(8,128)(2,1)S(1)}, bf16[128,16]{0,1:T(8,128)(2,1)S(1)}, u32[]{:S(2)}, u32[]{:S(2)}) collective-permute-start(bf16[128,16]{0,1:T(8,128)(2,1)S(1)} %get-tuple-element.20), channel_id=1, source_target_pairs={{0,15},{1,0},{2,1},{3,2},{4,3},{5,4},{6,5},{7,6},{8,7},{9,8},{10,9... | collective-permute-start | bytes 12296 | tf_op jit(solution)/shard_map/ppermute | solution.py:21
  98.9 44.3 %collective-permute-start.12 = (bf16[128,1433]{0,1:T(8,128)(2,1)}, bf16[128,1433]{0,1:T(8,128)(2,1)S(1)}, u32[]{:S(2)}, u32[]{:S(2)}) collective-permute-start(bf16[128,1433]{0,1:T(8,128)(2,1)} %get-tuple-element.13), channel_id=1, source_target_pairs={{0,15},{1,0},{2,1},{3,2},{4,3},{5,4},{6,5},{7,6},{8,7},{9,8},{10,9... | collective-permute-start | bytes 1100552 | tf_op jit(solution)/shard_map/ppermute | solution.py:34
  101.9 41.3 %collective-permute-start.15 = (bf16[128,1433]{0,1:T(8,128)(2,1)}, bf16[128,1433]{0,1:T(8,128)(2,1)}, u32[]{:S(2)}, u32[]{:S(2)}) collective-permute-start(bf16[128,1433]{0,1:T(8,128)(2,1)} %get-tuple-element.14), channel_id=1, source_target_pairs={{0,2},{1,3},{2,4},{3,5},{4,6},{5,7},{6,8},{7,9},{8,10},{9,11},{10,... | collective-permute-start | bytes 1100552 | tf_op jit(solution)/shard_map/ppermute | solution.py:34
  101.9 41.3 %collective-permute-start.14 = (bf16[128,1433]{0,1:T(8,128)(2,1)S(1)}, bf16[128,1433]{0,1:T(8,128)(2,1)}, u32[]{:S(2)}, u32[]{:S(2)}) collective-permute-start(bf16[128,1433]{0,1:T(8,128)(2,1)S(1)} %get-tuple-element.15), channel_id=1, source_target_pairs={{0,14},{1,15},{2,0},{3,1},{4,2},{5,3},{6,4},{7,5},{8,6},{9,7},{10,... | collective-permute-start | bytes 1100552 | tf_op jit(solution)/shard_map/ppermute | solution.py:34
  104.6 38.6 %collective-permute-start.13 = (bf16[128,1433]{0,1:T(8,128)(2,1)S(1)}, bf16[128,1433]{0,1:T(8,128)(2,1)}, u32[]{:S(2)}, u32[]{:S(2)}) collective-permute-start(bf16[128,1433]{0,1:T(8,128)(2,1)S(1)} %get-tuple-element.16), channel_id=1, source_target_pairs={{0,1},{1,2},{2,3},{3,4},{4,5},{5,6},{6,7},{7,8},{8,9},{9,10},{10,1... | collective-permute-start | bytes 1100552 | tf_op jit(solution)/shard_map/ppermute | solution.py:34
  108.8 9.5 %copy-start.3 = (bf16[1536,7]{0,1:T(8,128)(2,1)S(1)}, bf16[1536,7]{0,1:T(8,128)(2,1)}, u32[]{:S(2)}) copy-start(bf16[1536,7]{0,1:T(8,128)(2,1)} %param.13) | copy-start | bytes 64516
Sparse Core Ops, SparseCore 0:
  109.0 100.4 all-reduce.1
where the time goes:
time: 219 us; the launch traced here: 218 us
  local copies, waits for them, and re-layouts  45.1 us (21%)
  matrix products  42.7 us (19%)
  waiting for transfers between devices  42.3 us (19%)
  starting transfers between devices  26.3 us (12%)
  blocking collectives  24.2 us (11%)
  other arithmetic  23 us (11%)
  between operations  14.3 us (7%)
    psum x1, waiting for transfers between devices, device_step(): dw_first = lax.psum(contract_rows(z_first, grad_pre), 'nodes')  36.4 us
    psum x1, blocking collectives, device_step(): dw_second = lax.psum(contract_rows(z_second, grad_out), 'nodes')  24.2 us
    unnamed x25, local copies, waits for them, and re-layouts  19.8 us
    dot_general x6, matrix products, contract_rows(): lax.dot_general(left_rows, right_rows, (((0,), (0,)), ((), ())), preferre...  19.1 us
    scatter-add x2, other arithmetic, aggregate_back(): return inner_sum.at[send_idx.reshape(-1)].add(returned)  18.3 us
    ppermute x8, starting transfers between devices, aggregate_back(): lax.ppermute(outward[link * num_slots:(link + 1) * num_slots], 'nodes', s...  15.9 us
    dot_general x2, matrix products, aggregate(): jnp.dot(a_int, features, preferred_element_type=jnp.float32)  13.7 us
    ppermute x8, starting transfers between devices, halo_rows(): lax.ppermute(sent_rows[link], 'nodes', shift_pairs(axis_size, offset))  10.4 us
  transfers between devices with their start and end apart: 17, of which 2 were waited for; matrix products, arithmetic and copies ran while one was open for 37% of the time, Pallas kernels for 0%

commit v1 on v0

v1 whole, which is shorter than its diff:
```python
import functools

import jax
import jax.numpy as jnp
from jax import lax
from jax.experimental import pallas as pl
from jax.experimental.pallas import tpu as pltpu
from jax.sharding import PartitionSpec as P

MESH = pl.DeviceIdType.MESH
BF16 = jnp.bfloat16
F32 = jnp.float32
ROWS = 256
LANES = 128


def link_offsets(num_links):
    return [(link // 2 + 1) * (1 - 2 * (link % 2)) for link in range(num_links)]


def nn(left, right):
    return lax.dot_general(left, right, (((1,), (0,)), ((), ())), preferred_element_type=F32)


def nt(left, right):
    return lax.dot_general(left, right, (((1,), (1,)), ((), ())), preferred_element_type=F32)


def tn(left, right):
    return lax.dot_general(left, right, (((0,), (0,)), ((), ())), preferred_element_type=F32)


def halves(value):
    high = value.astype(BF16)
    return high, (value - high.astype(F32)).astype(BF16)


def chunks_of(total, size):
    return [(start, min(size, total - start)) for start in range(0, total, size)]


def round_up(value, multiple):
    return -(-value // multiple) * multiple


def graph_kernel(n, x_hbm, a_hbm, ah_hbm, idx_ref, w1_ref, w2_ref, g_ref,
                 t_ref, dw_ref,
                 x, a, ah, hot, send, recv, acc, z, g_send, g_recv, f_send, f_recv, part, part_in, total,
                 x_sem, a_sem, ah_sem, s_sem, r_sem, gs_sem, gr_sem, fs_sem, fr_sem, ps_sem, pr_sem, ts_sem, tr_sem):
    feats, nodes = x_hbm.shape
    num_links = idx_ref.shape[0]
    slots = idx_ref.shape[1]
    hidden = w1_ref.shape[0]
    classes = w2_ref.shape[0]
    offsets = link_offsets(num_links)
    steps = chunks_of(feats, ROWS)
    me = lax.axis_index("nodes")

    def peer(offset):
        return {"nodes": lax.rem(me + offset + n, n)}

    x_copies = [pltpu.make_async_copy(x_hbm.at[pl.ds(start, size)], x.at[pl.ds(start, size)], x_sem.at[c]) for c, (start, size) in enumerate(steps)]
    a_copy = pltpu.make_async_copy(a_hbm, a, a_sem)
    ah_copy = pltpu.make_async_copy(ah_hbm, ah, ah_sem)
    for copy in x_copies:
        copy.start()
    ah_copy.start()
    a_copy.start()

    barrier = pltpu.get_barrier_semaphore()
    for far in range(1, n):
        pl.semaphore_signal(barrier, inc=1, device_id=peer(far), device_id_type=MESH)

    row_pos = lax.broadcasted_iota(jnp.int32, (nodes, slots), 0)
    for link in range(num_links):
        hot[:, link * slots:(link + 1) * slots] = jnp.where(row_pos == idx_ref[link:link + 1, :], 1.0, 0.0).astype(BF16)

    pl.semaphore_wait(barrier, n - 1)

    x_sends = []
    for c, (start, size) in enumerate(steps):
        x_copies[c].wait()
        send[start:start + size, :] = nn(x[start:start + size, :], hot[...]).astype(BF16)
        for link, offset in enumerate(offsets):
            where = (pl.ds(start, size), pl.ds(link * slots, slots))
            copy = pltpu.make_async_remote_copy(send.at[where], recv.at[where], s_sem.at[c, link], r_sem.at[c, link], device_id=peer(offset), device_id_type=MESH)
            copy.start()
            x_sends.append(copy)

    def send_back(source, target, source_sem, target_sem):
        copies = []
        for link, offset in enumerate(offsets):
            where = (slice(None), pl.ds(link * slots, slots))
            copy = pltpu.make_async_remote_copy(source.at[where], target.at[where], source_sem.at[link], target_sem.at[link], device_id=peer(-offset), device_id_type=MESH)
            copy.start()
            copies.append(copy)
        return copies

    g_rows = g_ref[...]
    e_rows = tn(w2_ref[...], g_rows).astype(BF16)
    eg = jnp.concatenate([e_rows, g_rows, jnp.zeros((16 - classes, nodes), BF16)], axis=0)
    ah_copy.wait()
    outward = nn(eg, ah[...])
    g_send[...] = jnp.concatenate([outward[:hidden].astype(BF16).astype(F32), outward[hidden:hidden + 8]], axis=0)
    g_sends = send_back(g_send, g_recv, gs_sem, gr_sem)

    a_copy.wait()
    eg_sum = nn(eg, a[...])

    for c, (start, size) in enumerate(steps):
        acc[start:start + size, :] = nt(x[start:start + size, :], a[...])

    for copy in g_sends:
        copy.wait()
    g_high, g_low = halves(g_recv[hidden:, :])
    back = nt(jnp.concatenate([g_recv[:hidden, :].astype(BF16), g_high, g_low], axis=0), hot[...])
    d_rows = eg_sum[:hidden] + back[:hidden]
    u_rows = eg_sum[hidden:hidden + 8] + back[hidden:hidden + 8] + back[hidden + 8:hidden + 16]
    u_high, u_low = halves(u_rows)

    pre = jnp.zeros((hidden, nodes), F32)
    for c, (start, size) in enumerate(steps):
        for link in range(num_links):
            x_sends[c * num_links + link].wait()
        z_rows = (acc[start:start + size, :] + nt(recv[start:start + size, :], ah[...])).astype(BF16)
        z[start:start + size, :] = z_rows
        pre = pre + nn(w1_ref[:, start:start + size], z_rows)

    h_rows = jnp.maximum(pre, 0.0).astype(BF16)
    f_rows = jnp.where(h_rows.astype(F32) > 0.0, d_rows, 0.0).astype(BF16)

    f_send[...] = nn(f_rows, ah[...])
    f_sends = send_back(f_send, f_recv, fs_sem, fr_sem)

    dw = nt(f_rows, z[...])
    dw2 = nt(h_rows, u_high) + nt(h_rows, u_low)
    wide = part.shape[2]
    edge = wide - LANES
    for h in range(hidden):
        part[h, :, :feats] = dw[h:h + 1, :]
        part[h, :, edge:edge + 8] = dw2[h:h + 1, :]
    p_sends = []
    for far in range(1, n):
        to = lax.rem(me + far, n)
        copy = pltpu.make_async_remote_copy(part.at[to], part_in.at[far], ps_sem.at[far], pr_sem.at[far], device_id=peer(far), device_id_type=MESH)
        copy.start()
        p_sends.append(copy)

    t_rows = nn(f_rows, a[...])
    for copy in f_sends:
        copy.wait()
    f_high, f_low = halves(f_recv[...])
    f_back = nt(jnp.concatenate([f_high, f_low], axis=0), hot[...])
    t_rows = t_rows + f_back[:hidden] + f_back[hidden:]
    t_high, t_low = halves(t_rows)
    t_ref[...] = jnp.concatenate([t_high, t_low], axis=0)

    mine = part[me]
    for copy in p_sends:
        copy.wait()
    for far in range(1, n):
        mine = mine + part_in[far]
    total[me] = mine
    t_sends = []
    for far in range(1, n):
        copy = pltpu.make_async_remote_copy(total.at[me], total.at[me], ts_sem.at[far], tr_sem.at[far], device_id=peer(far), device_id_type=MESH)
        copy.start()
        t_sends.append(copy)
    for copy in t_sends:
        copy.wait()
    dw_ref[...] = total[...]


def grad_kernel(w1_ref, t_ref, dw_ref, out_ref, dw1_ref, dw2_ref):
    hidden, feats = dw1_ref.shape
    classes = dw2_ref.shape[0]
    w = w1_ref[...]
    out_ref[...] = tn(jnp.concatenate([w, w], axis=0), t_ref[...])

    @pl.when(pl.program_id(0) == 0)
    def _():
        edge = dw_ref.shape[2] - LANES
        for h in range(hidden):
            dw1_ref[h:h + 1, :] = dw_ref[h, :, :feats]
        tail = jnp.concatenate([dw_ref[h, :, edge:] for h in range(hidden)] + [jnp.zeros((LANES - hidden, LANES), F32)], axis=0)
        dw2_ref[...] = tail.T[:classes, :hidden]


def solution(mesh):
    n = mesh.shape["nodes"]
    row_spec = P(("graph", "nodes"), None)
    replicated = P(None, None)
    part_spec = P("graph", None)
    vmem = pl.BlockSpec(memory_space=pltpu.VMEM)
    hbm = pl.BlockSpec(memory_space=pl.ANY)

    def device_step(node_feats, a_int, a_halo, send_idx, w_first, w_second, grad_out):
        nodes, feats = node_feats.shape
        num_links, slots = send_idx.shape
        hidden, classes = w_second.shape
        assert hidden == n and classes <= 8
        halo = num_links * slots
        padded = round_up(feats, 16)
        wide = round_up(feats, LANES) + LANES
        num_steps = len(chunks_of(feats, ROWS))
        w1 = w_first.T
        dma = pltpu.SemaphoreType.DMA
        t_parts, dw = pl.pallas_call(
            functools.partial(graph_kernel, n),
            out_shape=(jax.ShapeDtypeStruct((2 * hidden, nodes), BF16), jax.ShapeDtypeStruct((hidden, 1, wide), F32)),
            in_specs=[hbm, hbm, hbm, vmem, vmem, vmem, vmem],
            out_specs=(vmem, vmem),
            scratch_shapes=[
                pltpu.VMEM((feats, nodes), BF16),
                pltpu.VMEM((nodes, nodes), BF16),
                pltpu.VMEM((nodes, halo), BF16),
                pltpu.VMEM((nodes, halo), BF16),
                pltpu.VMEM((feats, halo), BF16),
                pltpu.VMEM((feats, halo), BF16),
                pltpu.VMEM((feats, nodes), F32),
                pltpu.VMEM((feats, nodes), BF16),
                pltpu.VMEM((hidden + 8, halo), F32),
                pltpu.VMEM((hidden + 8, halo), F32),
                pltpu.VMEM((hidden, halo), F32),
                pltpu.VMEM((hidden, halo), F32),
                pltpu.VMEM((hidden, 1, wide), F32),
                pltpu.VMEM((n, 1, wide), F32),
                pltpu.VMEM((hidden, 1, wide), F32),
                dma((num_steps,)), dma, dma,
                dma((num_steps, num_links)), dma((num_steps, num_links)),
                dma((num_links,)), dma((num_links,)), dma((num_links,)), dma((num_links,)),
                dma((n,)), dma((n,)), dma((n,)), dma((n,)),
            ],
            compiler_params=pltpu.CompilerParams(collective_id=0, has_side_effects=True, vmem_limit_bytes=60 * 1024 * 1024),
            name="graph_kernel",
        )(node_feats.T, a_int, a_halo, send_idx, w1, w_second.T, grad_out.T)

        block = 256
        grads, dw1, dw2 = pl.pallas_call(
            grad_kernel,
            grid=(pl.cdiv(feats, block),),
            out_shape=(jax.ShapeDtypeStruct((feats, nodes), F32), jax.ShapeDtypeStruct((hidden, feats), F32), jax.ShapeDtypeStruct((classes, hidden), F32)),
            in_specs=[
                pl.BlockSpec((hidden, block), lambda i: (0, i)),
                pl.BlockSpec((2 * hidden, nodes), lambda i: (0, 0)),
                pl.BlockSpec((hidden, 1, wide), lambda i: (0, 0, 0)),
            ],
            out_specs=(
                pl.BlockSpec((block, nodes), lambda i: (i, 0)),
                pl.BlockSpec((hidden, feats), lambda i: (0, 0)),
                pl.BlockSpec((classes, hidden), lambda i: (0, 0)),
            ),
            name="grad_kernel",
        )(w1, t_parts, dw)
        return dw1.T, dw2.T, grads.T

    return jax.shard_map(device_step, mesh=mesh, in_specs=(row_spec, row_spec, row_spec, row_spec, replicated, replicated, row_spec), out_specs=(part_spec, part_spec, row_spec), check_vma=False)
```

time: 219 us -> 52.8 us (0.24)
  Pallas kernels: 0 us -> 51.9 us
  local copies, waits for them, and re-layouts: 45.1 us -> 0 us
  matrix products: 42.7 us -> 0 us
  waiting for transfers between devices: 42.3 us -> 0 us
  starting transfers between devices: 26.3 us -> 0 us
  blocking collectives: 24.2 us -> 0 us
  other arithmetic: 23 us -> 0 us
  between operations: 14.3 us -> 0.64 us
    pallas_call x0 -> x2, Pallas kernels: none -> 51.9 us  [the longest x1 45.7 us: device_step(): pl.pallas_call(functools.partial(graph_kernel, n), out_shape=(jax.ShapeDt...]
    dot_general x12 -> x0, matrix products: 42.7 us -> none  [the longest x6 19.1 us: contract_rows(): lax.dot_general(left_rows, right_rows, (((0,), (0,)), ((), ())), preferre...]
    psum x1 -> x0, waiting for transfers between devices: 36.4 us -> none  [device_step(): dw_first = lax.psum(contract_rows(z_first, grad_pre), 'nodes')]
    ppermute x16 -> x0, starting transfers between devices: 26.2 us -> none  [the longest x8 15.9 us: aggregate_back(): lax.ppermute(outward[link * num_slots:(link + 1) * num_slots], 'nodes', s...]
    psum x1 -> x0, blocking collectives: 24.2 us -> none  [device_step(): dw_second = lax.psum(contract_rows(z_second, grad_out), 'nodes')]
    unnamed x25 -> x0, local copies, waits for them, and re-layouts: 19.8 us -> none
    scatter-add x2 -> x0, other arithmetic: 18.3 us -> none  [aggregate_back(): return inner_sum.at[send_idx.reshape(-1)].add(returned)]
    dot_general x2 -> x0, local copies, waits for them, and re-layouts: 9.77 us -> none  [contract_rows(): lax.dot_general(left_rows, right_rows, (((0,), (0,)), ((), ())), preferre...]
  transfers between devices with their start and end apart: 17 -> 0, of which waited for: 2 -> 0; matrix products, arithmetic and copies ran while one was open for 37% -> 0% of each run, Pallas kernels for 0% -> 0%
where the time goes in v1:
time: 52.8 us; the launch traced here: 52.5 us
  Pallas kernels  51.9 us (98%)
  between operations  0.64 us (1%)
    pallas_call x1, Pallas kernels, device_step(): pl.pallas_call(functools.partial(graph_kernel, n), out_shape=(jax.ShapeDt...  45.7 us
    pallas_call x1, Pallas kernels, device_step(): pl.pallas_call(grad_kernel, grid=(pl.cdiv(feats, block),), out_shape=(jax...  6.16 us

profile of v1, /device:TPU:21, one launch (start us, length us, event | category | flops | bytes accessed | tf_op | source)
XLA Modules:
  0.0 52.5 jit_solution(16276472691719074168)
XLA Ops:
  0.6 45.7 %graph_kernel.1 = (bf16[32,1536]{1,0:T(8,128)(2,1)}, f32[16,1,1664]{2,1,0:T(1,128)}) custom-call(bf16[1433,1536]{1,0:T(8,128)(2,1)} %bitcast.7, bf16[1536,1536]{1,0:T(8,128)(2,1)} %a_hbm.1, bf16[1536,512]{1,0:T(8,128)(2,1)} %ah_hbm.1, s32[4,128]{1,0:T(4,128)} %idx_ref.1, bf16[16,1433]{1,0:T(8,128)(2,1)} %bitcast.8, bf16[7,16]{1,0:T(8,128)(2,1)} %bitcast.11, ...), custom_call_target="tpu_custom_call" | custom-call | tf_op jit(solution)/shard_map/graph_kernel/pallas_call | solution.py:208
  46.4 6.2 %grad_kernel.1 = (f32[1433,1536]{1,0:T(8,128)}, f32[16,1433]{1,0:T(8,128)}, f32[7,16]{1,0:T(8,128)}) custom-call(bf16[16,1433]{1,0:T(8,128)(2,1)} %bitcast.9, bf16[32,1536]{1,0:T(8,128)(2,1)} %get-tuple-element.8.t_ref, f32[16,1,1664]{2,1,0:T(1,128)} %get-tuple-element.9.dw_ref), custom_call_target="tpu_custom_call" | custom-call | tf_op jit(solution)/shard_map/grad_kernel/pallas_call | solution.py:239
